TPU v7x, 32 devices: a whole 2x2x4 slice. The times are simulated.
32 devices in a mesh: seq: 16 (over z, x, core), head: 2 (over y).
Axes of the slice: x: 2, y: 2, z: 4, core: 2. Of those that a mesh axis runs over, the one named last changes fastest.
Arguments:
- hidden: bfloat16 [4608, 8192], P('seq'), may hold values from -6 to 6
- norm_gain: bfloat16 [8192], replicated, may hold values from 0.099609375 to 1.8984375
- w_query: bfloat16 [8192, 1024], P('seq', 'head'), may hold values from -0.125 to 0.125
- w_key: bfloat16 [8192, 256], P('seq', 'head'), may hold values from -0.125 to 0.125
- w_value: bfloat16 [8192, 256], P('seq', 'head'), may hold values from -0.0625 to 0.0625
- bias_query: bfloat16 [1024], P('head'), may hold values from -3 to 3
- bias_key: bfloat16 [256], P('head'), may hold values from -200 to 200
- bias_value: bfloat16 [256], P('head'), may hold values from -3 to 3
- w_out: bfloat16 [1024, 8192], P('head', 'seq'), may hold values from -0.1875 to 0.1875
Outputs:
- attn_out: bfloat16 [4608, 8192], P(('seq', 'head'))
All inputs are finite; a program needn't handle non-finite values.
Results may differ from a plain program's by a relative error of at most 0.014.
The roundings to bfloat16 on the way count: a program that leaves them out, or rounds other values in their place, can miss the bound.
Values may be sent and summed in bfloat16 or wider, within the bound.
No kernel may reach another device: no remote copies, remote signals or barrier semaphores. Data moves between devices by JAX's collectives and lax.ppermute only.
A program may use at most 192 MiB of HBM per device.

v0:
```python
import jax
import jax.numpy as jnp
from jax import lax
from jax.sharding import PartitionSpec as P

HEAD_DIM = 128
ROPE_BASE = 1000000.0
EPSILON = 1e-06


def rotary(values, positions):
    half_dim = values.shape[-1] // 2
    freq = ROPE_BASE ** (-2.0 * jnp.arange(half_dim, dtype=jnp.float32) / values.shape[-1])
    angles = positions.astype(jnp.float32)[:, None, None] * freq[None, None, :]
    cosine = jnp.cos(angles)
    sine = jnp.sin(angles)
    first = values[..., :half_dim]
    second = values[..., half_dim:]
    return jnp.concatenate(
        [first * cosine - second * sine, second * cosine + first * sine], axis=-1
    )


def local(hidden, norm_gain, w_query, w_key, w_value, bias_query, bias_key, bias_value, w_out):
    row_count = hidden.shape[0]
    head_count = w_query.shape[1] // HEAD_DIM
    first_row = lax.axis_index("seq") * row_count
    last_row = first_row + row_count - 1
    positions = first_row + jnp.arange(row_count, dtype=jnp.int32)
    widened = hidden.astype(jnp.float32)
    inverse = lax.rsqrt(jnp.mean(widened * widened, axis=-1, keepdims=True) + EPSILON)
    normed = (widened * inverse * norm_gain.astype(jnp.float32)).astype(jnp.bfloat16)
    query = jnp.dot(
        normed,
        lax.all_gather(w_query, "seq", axis=0, tiled=True),
        preferred_element_type=jnp.float32,
    )
    keys = jnp.dot(
        normed, lax.all_gather(w_key, "seq", axis=0, tiled=True), preferred_element_type=jnp.float32
    )
    values = jnp.dot(
        normed,
        lax.all_gather(w_value, "seq", axis=0, tiled=True),
        preferred_element_type=jnp.float32,
    )
    query = query + bias_query.astype(jnp.float32)
    keys = keys + bias_key.astype(jnp.float32)
    values = values + bias_value.astype(jnp.float32)
    query = rotary(query.reshape(row_count, head_count, HEAD_DIM), positions).astype(jnp.bfloat16)
    keys = (
        rotary(keys.reshape(row_count, 1, HEAD_DIM), positions)
        .reshape(row_count, HEAD_DIM)
        .astype(jnp.bfloat16)
    )
    values = values.astype(jnp.bfloat16)
    query_heads = query.transpose(1, 0, 2)
    scaling = HEAD_DIM ** (-0.5)
    initial = (
        jnp.full((head_count, row_count), -1e30, jnp.float32),
        jnp.zeros((head_count, row_count), jnp.float32),
        jnp.zeros((head_count, row_count, HEAD_DIM), jnp.float32),
    )
    key_piece = lax.all_gather(keys, "seq", axis=0, tiled=True)
    value_piece = lax.all_gather(values, "seq", axis=0, tiled=True)

    def update(state):
        highest, total, summed = state
        scores = (
            jnp.einsum("hqd,kd->hqk", query_heads, key_piece, preferred_element_type=jnp.float32)
            * scaling
        )
        key_positions = jnp.arange(key_piece.shape[0], dtype=jnp.int32)
        allowed = positions[:, None] >= key_positions[None, :]
        scores = jnp.where(allowed[None], scores, -jnp.inf)
        new_high = jnp.maximum(highest, jnp.max(scores, axis=-1))
        probs = jnp.exp(scores - new_high[..., None])
        total = jnp.sum(probs, axis=-1)
        mixed = jnp.einsum(
            "hqk,kd->hqd",
            probs.astype(jnp.bfloat16),
            value_piece,
            preferred_element_type=jnp.float32,
        )
        return (new_high, total, mixed)

    def unchanged(state):
        return state

    highest, total, summed = lax.cond(jnp.int32(0) <= last_row, update, unchanged, initial)
    attended = (summed / total[..., None]).astype(jnp.bfloat16)
    attended = attended.transpose(1, 0, 2).reshape(row_count, head_count * HEAD_DIM)
    partial_out = jnp.dot(
        attended,
        lax.all_gather(w_out, "seq", axis=1, tiled=True),
        preferred_element_type=jnp.float32,
    )
    result = lax.psum_scatter(
        partial_out.astype(jnp.bfloat16), "head", scatter_dimension=0, tiled=True
    )
    return result


def solution(mesh):
    in_specs = (
        P("seq", None),
        P(),
        P("seq", "head"),
        P("seq", "head"),
        P("seq", "head"),
        P("head"),
        P("head"),
        P("head"),
        P("head", "seq"),
    )
    out_specs = P(("seq", "head"), None)
    return jax.shard_map(local, mesh=mesh, in_specs=in_specs, out_specs=out_specs, check_vma=False)
```

profile of v0, /device:TPU:0, one launch (start us, length us, event | category | flops | bytes accessed | tf_op | source)
XLA Modules:
  0.0 401.3 jit_solution(17232137514900571910)
XLA Ops:
  6.5 0.0 all-gather.10.cloned.1.call-start
  6.5 0.7 all-gather.10.cloned.1.call-update
  7.3 0.0 all-gather.12.cloned.1.call-start
  7.3 0.7 all-gather.12.cloned.1.call-update
  8.0 0.0 all-gather.8.cloned.1.call-start
  8.1 0.7 all-gather.8.cloned.1.call-update
  8.7 0.0 all-gather.18.cloned.1.call-start
  8.8 0.7 convert_element_type.48
  9.5 0.7 convert_element_type.52
  10.2 3.4 fusion.11
  13.5 0.0 copy-start.1
  13.6 40.1 %all-gather.10.cloned.1.call-done = bf16[8192,128]{1,0:T(8,128)(2,1)} async-done(((bf16[512,128]{1,0:T(8,128)(2,1)}), bf16[8192,128]{1,0:T(8,128)(2,1)}) %all-gather.10.cloned.1.call-update) | async-done | bytes 2097168 | tf_op jit(solution)/shard_map/all_gather | solution.py:39
  53.7 4.6 %fusion.14 = f32[288,1,128]{2,0,1:T(8,128)S(1)} fusion(bf16[8192,128]{1,0:T(8,128)(2,1)} %all-gather.10.cloned.1.call-done, f32[128]{0:T(128)S(1)} %convert_element_type.52, bf16[288,8192]{1,0:T(8,128)(2,1)} %param.11, f32[8192]{0:T(1024)S(1)} %convert_element_type.48, f32[288]{0:T(512)S(1)} %add_rsqrt_fusion), kind=kOutput, calls=%fused_computation.24 | convolution fusion | flops 613453824 | bytes 6997632 | tf_op jit(solution)/shard_map/dot_general | solution.py:38
  58.3 0.0 copy-start
  58.3 0.7 fusion.24
  58.9 0.7 pad_maximum_fusion
  59.7 0.0 all-gather.18.cloned.1.call-update
  59.7 0.0 all-gather.14.cloned.1.call-start
  59.7 0.0 copy-done.1
  59.8 36.3 %all-gather.12.cloned.1.call-done = bf16[8192,128]{1,0:T(8,128)(2,1)} async-done(((bf16[512,128]{1,0:T(8,128)(2,1)}), bf16[8192,128]{1,0:T(8,128)(2,1)}) %all-gather.12.cloned.1.call-update) | async-done | bytes 2097168 | tf_op jit(solution)/shard_map/all_gather | solution.py:43
  96.1 5.1 %fusion.15 = bf16[288,128]{1,0:T(8,128)(2,1)} fusion(bf16[8192,128]{1,0:T(8,128)(2,1)} %all-gather.12.cloned.1.call-done, f32[128]{0:T(128)S(1)} %convert_element_type.54, bf16[288,8192]{1,0:T(8,128)(2,1)} %param.11, f32[8192]{0:T(1024)S(1)} %convert_element_type.48, f32[288]{0:T(512)S(1)} %add_rsqrt_fusion), kind=kOutput, calls=%fused_computation.25 | convolution fusion | flops 613490688 | bytes 6923904 | tf_op jit(solution)/shard_map/dot_general | solution.py:41
  101.2 0.0 all-gather.14.cloned.1.call-update
  101.2 0.0 all-gather.16.cloned.1.call-start
  101.3 0.5 all-gather.16.cloned.1.call-update
  101.8 0.2 reduce-scatter.2.cloned.1.call-start
  102.0 0.0 copy-done
  102.1 0.6 multiply_cosine_fusion.1
  102.7 68.6 %all-gather.8.cloned.1.call-done = bf16[8192,512]{1,0:T(8,128)(2,1)} async-done(((bf16[512,512]{1,0:T(8,128)(2,1)}), bf16[8192,512]{1,0:T(8,128)(2,1)}) %all-gather.8.cloned.1.call-update) | async-done | bytes 8388624 | tf_op jit(solution)/shard_map/all_gather | solution.py:35
  171.3 7.0 %convolution_add_fusion = f32[288,512]{1,0:T(8,128)S(1)} fusion(bf16[8192,512]{1,0:T(8,128)(2,1)} %all-gather.8.cloned.1.call-done, f32[512]{0:T(512)S(1)} %convert_element_type.50, bf16[288,8192]{1,0:T(8,128)(2,1)} %param.11, f32[8192]{0:T(1024)S(1)} %convert_element_type.48, f32[288]{0:T(512)S(1)} %add_rsqrt_fusion), kind=kOutput, calls=%fused_computation.21 | convolution fusion | flops 2425503744 | bytes 13732992 | tf_op jit(solution)/shard_map/dot_general | solution.py:33
  178.3 0.2 reshape.159
  178.6 0.4 fusion.30
  178.9 0.2 subtract_convert_fusion
  179.1 0.2 maximum_bitcast_fusion
  179.3 31.1 %all-gather.18.cloned.1.call-done = bf16[4608,1,128]{2,0,1:T(8,128)(2,1)} async-done(((bf16[288,1,128]{2,0,1:T(8,128)(2,1)}), bf16[4608,1,128]{2,0,1:T(8,128)(2,1)}) %all-gather.18.cloned.1.call-update) | async-done | bytes 1179664 | tf_op jit(solution)/shard_map/all_gather | solution.py:63
  210.3 39.3 %all-gather.14.cloned.1.call-done = bf16[4608,128]{1,0:T(8,128)(2,1)} async-done(((bf16[288,128]{1,0:T(8,128)(2,1)}), bf16[4608,128]{1,0:T(8,128)(2,1)}) %all-gather.14.cloned.1.call-update) | async-done | bytes 1179664 | tf_op jit(solution)/shard_map/all_gather | solution.py:64
  249.7 19.5 %conditional.1 = (f32[4,288]{1,0:T(4,128)S(1)}, f32[4,288,128]{2,1,0:T(8,128)S(1)}) conditional(s32[]{:T(128)} %convert_element_type.46, () %tuple.13, (s32[]{:T(128)}, s32[288]{0:T(512)S(1)}, bf16[4,288,128]{2,1,0:T(8,128)(2,1)S(1)}, bf16[4608,128]{1,0:T(8,128)(2,1)}, bf16[4608,128]{1,0:T(8,128)(2,1)}) %tuple.36), branch_computations={%region_1.0_spmd, %region_2.5_spmd} | conditional | flops 2777627648 | bytes 72284560 | solution.py:89
  249.7 0.8 iota_compare_fusion
  250.5 5.5 %fusion = (f32[4,288]{1,0:T(4,128)S(1)}, f32[4,288,4608]{2,1,0:T(8,128)S(1)}) fusion(pred[288,4608]{1,0:T(8,128)(4,1)S(1)} %iota_compare_fusion, bf16[4,288,128]{2,1,0:T(8,128)(2,1)S(1)} %get-tuple-element.19, bf16[4608,128]{1,0:T(8,128)(2,1)} %get-tuple-element.20), kind=kOutput, calls=%fused_computation.2 | convolution fusion | flops 1374878592 | bytes 24039936 | tf_op jit(solution)/shard_map/cond/branch_1_fun/hqd,kd->hqk/dot_general | solution.py:69
  255.9 6.6 %fusion.3 = f32[4,288,128]{2,1,0:T(8,128)S(1)} fusion(f32[4,288,4608]{2,1,0:T(8,128)S(1)} %get-tuple-element.27, f32[4,288]{1,0:T(4,128)S(1)} %broadcast_maximum_fusion, pred[288,4608]{1,0:T(8,128)(4,1)S(1)} %iota_compare_fusion, bf16[4608,128]{1,0:T(8,128)(2,1)} %get-tuple-element.21), kind=kOutput, calls=%fused_computation.5 | convolution fusion | flops 1380188160 | bytes 24334848 | tf_op jit(solution)/shard_map/cond/branch_1_fun/hqk,kd->hqd/dot_general | solution.py:78
  262.6 6.6 %fusion.2 = f32[4,288]{1,0:T(4,128)S(1)} fusion(f32[4,288,4608]{2,1,0:T(8,128)S(1)} %get-tuple-element.27, f32[4,288]{1,0:T(4,128)S(1)} %broadcast_maximum_fusion, pred[288,4608]{1,0:T(8,128)(4,1)S(1)} %iota_compare_fusion), kind=kLoop, calls=%fused_computation.4 | loop fusion | flops 21232512 | bytes 22569984 | tf_op jit(solution)/shard_map/cond/branch_1_fun/reduce_sum | solution.py:77
  269.2 59.2 %all-gather.16.cloned.1.call-done = bf16[512,8192]{1,0:T(8,128)(2,1)} async-done(((bf16[512,512]{1,0:T(8,128)(2,1)}), bf16[512,8192]{1,0:T(8,128)(2,1)}) %all-gather.16.cloned.1.call-update) | async-done | bytes 8388624 | tf_op jit(solution)/shard_map/all_gather | solution.py:94
  328.3 7.7 %convolution_convert_fusion = bf16[288,8192]{1,0:T(8,128)(2,1)} fusion(bf16[512,8192]{1,0:T(8,128)(2,1)} %all-gather.16.cloned.1.call-done, f32[4,288,128]{2,1,0:T(8,128)S(1)} %get-tuple-element.24, f32[4,288]{1,0:T(4,128)S(1)} %get-tuple-element.25), kind=kOutput, calls=%fused_computation.17 | convolution fusion | flops 2418573312 | bytes 13701632 | tf_op jit(solution)/shard_map/dot_general | solution.py:92
  336.0 0.0 reduce-scatter.2.cloned.1.call-update
  336.1 58.4 %reduce-scatter.2.cloned.1.call-done = bf16[144,8192]{1,0:T(8,128)(2,1)} async-done(((bf16[288,8192]{1,0:T(8,128)(2,1)}), bf16[144,8192]{1,0:T(8,128)(2,1)}) %reduce-scatter.2.cloned.1.call-update) | async-done | bytes 2359312 | tf_op jit(solution)/shard_map/reduce_scatter | solution.py:97
  (8 shorter events, 0.0 us)
Async XLA Ops:
  6.5 47.2 %all-gather.10.cloned.1.call-start = ((), (), s32[]{:S(2)}) async-start(), calls=%async_computation.2 | async-start | bytes 2228224 | tf_op jit(solution)/shard_map/all_gather | solution.py:39
  7.3 88.8 %all-gather.12.cloned.1.call-start = ((), (), s32[]{:S(2)}) async-start(), calls=%async_computation.3 | async-start | bytes 2228224 | tf_op jit(solution)/shard_map/all_gather | solution.py:43
  8.0 163.3 %all-gather.8.cloned.1.call-start = ((), (), s32[]{:S(2)}) async-start(), calls=%async_computation.1 | async-start | bytes 8912896 | tf_op jit(solution)/shard_map/all_gather | solution.py:35
  8.7 201.6 %all-gather.18.cloned.1.call-start = ((), (), s32[]{:S(2)}) async-start(), calls=%async_computation.7 | async-start | bytes 1253376 | tf_op jit(solution)/shard_map/all_gather | solution.py:63
  13.5 46.2 %copy-start.1 = (bf16[128]{0:T(256)(128)(2,1)S(1)}, bf16[128]{0:T(256)(128)(2,1)}, u32[]{:S(2)}) copy-start(bf16[128]{0:T(256)(128)(2,1)} %param.18) | copy-start | bytes 772
  58.3 43.8 %copy-start = (bf16[512]{0:T(512)(128)(2,1)S(1)}, bf16[512]{0:T(512)(128)(2,1)}, u32[]{:S(2)}) copy-start(bf16[512]{0:T(512)(128)(2,1)} %param.16) | copy-start | bytes 3076
  59.7 190.0 %all-gather.14.cloned.1.call-start = ((), (), s32[]{:S(2)}) async-start(), calls=%async_computation.4 | async-start | bytes 1253376 | tf_op jit(solution)/shard_map/all_gather | solution.py:64
  101.2 227.1 %all-gather.16.cloned.1.call-start = ((), (), s32[]{:S(2)}) async-start(), calls=%async_computation.5 | async-start | bytes 8912896 | tf_op jit(solution)/shard_map/all_gather | solution.py:94
  101.8 292.6 %reduce-scatter.2.cloned.1.call-start = ((), (), s32[]{:S(2)}) async-start(), calls=%async_computation.6 | async-start | bytes 7077888 | tf_op jit(solution)/shard_map/reduce_scatter | solution.py:97
Sparse Core Ops, SparseCore 0:
  9.5 44.1 all-gather.9
  55.9 40.1 all-gather.11
  98.2 73.0 all-gather.7
  173.4 36.8 all-gather.17
  212.5 37.1 all-gather.13
  251.7 76.5 all-gather.15
  336.2 58.2 reduce-scatter.1
where the time goes:
time: 402 us; the launch traced here: 401 us
  waiting for transfers between devices  336 us (84%)
  matrix products  36.6 us (9%)
  other arithmetic  14.4 us (4%)
  between operations  13.6 us (3%)
    all_gather x1, waiting for transfers between devices, local(): lax.all_gather(w_query, 'seq', axis=0, tiled=True)  68.6 us
    all_gather x1, waiting for transfers between devices, local(): lax.all_gather(w_out, 'seq', axis=1, tiled=True)  59.2 us
    reduce_scatter x1, waiting for transfers between devices, local(): lax.psum_scatter(partial_out.astype(jnp.bfloat16), 'head', scatter_dimens...  58.4 us
    all_gather x1, waiting for transfers between devices, local(): lax.all_gather(w_key, 'seq', axis=0, tiled=True)  40.1 us
    all_gather x1, waiting for transfers between devices, local(): value_piece = lax.all_gather(values, 'seq', axis=0, tiled=True)  39.3 us
    all_gather x1, waiting for transfers between devices, local(): lax.all_gather(w_value, 'seq', axis=0, tiled=True)  36.3 us
    all_gather x1, waiting for transfers between devices, local(): key_piece = lax.all_gather(keys, 'seq', axis=0, tiled=True)  31.1 us
  transfers between devices with their start and end apart: 7, of which 7 were waited for; matrix products, arithmetic and copies ran while one was open for 11% of the time, Pallas kernels for 0%

commit v1 on v0

--- a/solution.py
+++ b/solution.py
@@ -60,7 +60,16 @@
         jnp.zeros((head_count, row_count), jnp.float32),
         jnp.zeros((head_count, row_count, HEAD_DIM), jnp.float32),
     )
-    key_piece = lax.all_gather(keys, "seq", axis=0, tiled=True)
+    ways = lax.axis_size("seq")
+    up = [(d, (d + 1) % ways) for d in range(ways)]
+    down = [(d, (d - 1) % ways) for d in range(ways)]
+    earlier, later = ([keys], [keys])
+    for _ in range(ways // 2):
+        earlier.append(lax.ppermute(earlier[-1], "seq", up))
+    for _ in range((ways - 1) // 2):
+        later.append(lax.ppermute(later[-1], "seq", down))
+    line = jnp.concatenate([*earlier[::-1], *later[1:]], axis=0)
+    key_piece = jnp.roll(line, (lax.axis_index("seq") - ways // 2) * keys.shape[0], axis=0)
     value_piece = lax.all_gather(values, "seq", axis=0, tiled=True)
 
     def update(state):

time: 402 us -> 369 us (0.918)
  waiting for transfers between devices: 336 us -> 252 us
  starting transfers between devices: 0.42 us -> 32.2 us
  local copies, waits for them, and re-layouts: 0.59 us -> 21 us
    all_gather x1, waiting for transfers between devices: 68.6 us -> 0.01 us  [local(): lax.all_gather(w_query, 'seq', axis=0, tiled=True)]
    ppermute x0 -> x15, starting transfers between devices: none -> 32 us  [the longest x7 31.7 us: local(): later.append(lax.ppermute(later[-1], 'seq', down))]
    all_gather x1 -> x0, waiting for transfers between devices: 31.1 us -> none  [local(): key_piece = lax.all_gather(keys, 'seq', axis=0, tiled=True)]
    ppermute x0 -> x15, waiting for transfers between devices: none -> 26.9 us  [the longest x8 23.1 us: local(): earlier.append(lax.ppermute(earlier[-1], 'seq', up))]
    unnamed x4 -> x35, local copies, waits for them, and re-layouts: 0.01 us -> 19.8 us
    all_gather x1, waiting for transfers between devices: 39.3 us -> 28 us  [local(): value_piece = lax.all_gather(values, 'seq', axis=0, tiled=True)]
  transfers between devices with their start and end apart: 7 -> 21, of which waited for: 7 -> 16; matrix products, arithmetic and copies ran while one was open for 11% -> 17% of each run, Pallas kernels for 0% -> 0%
where the time goes in v1:
time: 369 us
  waiting for transfers between devices  252 us (68%)
  matrix products  36.9 us (10%)
  starting transfers between devices  32.2 us (9%)
  local copies, waits for them, and re-layouts  21 us (6%)
  other arithmetic  13.8 us (4%)
  between operations  13.6 us (4%)
    all_gather x1, waiting for transfers between devices, local(): lax.all_gather(w_out, 'seq', axis=1, tiled=True)  58.9 us
    reduce_scatter x1, waiting for transfers between devices, local(): lax.psum_scatter(partial_out.astype(jnp.bfloat16), 'head', scatter_dimens...  58.4 us
    all_gather x1, waiting for transfers between devices, local(): lax.all_gather(w_value, 'seq', axis=0, tiled=True)  40.2 us
    all_gather x1, waiting for transfers between devices, local(): lax.all_gather(w_key, 'seq', axis=0, tiled=True)  36.5 us
    ppermute x7, starting transfers between devices, local(): later.append(lax.ppermute(later[-1], 'seq', down))  31.7 us
    all_gather x1, waiting for transfers between devices, local(): value_piece = lax.all_gather(values, 'seq', axis=0, tiled=True)  28 us
    ppermute x8, waiting for transfers between devices, local(): earlier.append(lax.ppermute(earlier[-1], 'seq', up))  23.1 us
    unnamed x35, local copies, waits for them, and re-layouts  19.8 us
  transfers between devices with their start and end apart: 21, of which 16 were waited for; matrix products, arithmetic and copies ran while one was open for 17% of the time, Pallas kernels for 0%

profile of v1, /device:TPU:0, one launch (start us, length us, event | category | flops | bytes accessed | tf_op | source)
XLA Modules:
  0.0 369.1 jit_solution(4852879712023571415)
XLA Ops:
  6.5 0.7 all-gather.10.cloned.1.call-update
  7.3 0.7 all-gather.6.cloned.1.call-update
  8.1 0.7 all-gather.8.cloned.1.call-update
  8.8 0.7 convert_element_type.51
  9.5 0.7 convert_element_type.57
  10.2 3.4 fusion.13
  13.5 40.2 %all-gather.10.cloned.1.call-done = bf16[8192,128]{1,0:T(8,128)(2,1)} async-done(((bf16[512,128]{1,0:T(8,128)(2,1)}), bf16[8192,128]{1,0:T(8,128)(2,1)}) %all-gather.10.cloned.1.call-update) | async-done | bytes 2097168 | tf_op jit(solution)/shard_map/all_gather | solution.py:43
  53.7 5.2 %fusion.17 = bf16[288,128]{1,0:T(8,128)(2,1)} fusion(bf16[8192,128]{1,0:T(8,128)(2,1)} %all-gather.10.cloned.1.call-done, f32[128]{0:T(128)S(1)} %convert_element_type.57, bf16[288,8192]{1,0:T(8,128)(2,1)} %param.11, f32[8192]{0:T(1024)S(1)} %convert_element_type.51, f32[288]{0:T(512)S(1)} %add_rsqrt_fusion), kind=kOutput, calls=%fused_computation.27 | convolution fusion | flops 613490688 | bytes 6923904 | tf_op jit(solution)/shard_map/dot_general | solution.py:41
  59.6 36.5 %all-gather.6.cloned.1.call-done = bf16[8192,128]{1,0:T(8,128)(2,1)} async-done(((bf16[512,128]{1,0:T(8,128)(2,1)}), bf16[8192,128]{1,0:T(8,128)(2,1)}) %all-gather.6.cloned.1.call-update) | async-done | bytes 2097168 | tf_op jit(solution)/shard_map/all_gather | solution.py:39
  96.1 4.6 %fusion.16 = f32[288,1,128]{2,0,1:T(8,128)S(1)} fusion(bf16[8192,128]{1,0:T(8,128)(2,1)} %all-gather.6.cloned.1.call-done, f32[128]{0:T(128)S(1)} %convert_element_type.53, bf16[288,8192]{1,0:T(8,128)(2,1)} %param.11, f32[8192]{0:T(1024)S(1)} %convert_element_type.51, f32[288]{0:T(512)S(1)} %add_rsqrt_fusion), kind=kOutput, calls=%fused_computation.26 | convolution fusion | flops 613453824 | bytes 6997632 | tf_op jit(solution)/shard_map/dot_general | solution.py:38
  100.6 0.7 fusion.26
  101.7 6.3 %collective-permute-done = bf16[288,128]{1,0:T(8,128)(2,1)S(1)} collective-permute-done((bf16[288,128]{1,0:T(8,128)(2,1)S(1)}, bf16[288,128]{1,0:T(8,128)(2,1)S(1)}, u32[]{:S(2)}, u32[]{:S(2)}) %collective-permute-start) | collective-permute-done | bytes 73760 | tf_op jit(solution)/shard_map/ppermute | solution.py:68
  107.9 4.4 %collective-permute-start.8 = (bf16[288,128]{1,0:T(8,128)(2,1)S(1)}, bf16[288,128]{1,0:T(8,128)(2,1)S(1)}, u32[]{:S(2)}, u32[]{:S(2)}) collective-permute-start(bf16[288,128]{1,0:T(8,128)(2,1)S(1)} %maximum_bitcast_fusion.1), channel_id=1, source_target_pairs={{0,30},{2,0},{4,2},{6,4},{8,6},{10,8},{12,10},{14,12},{16,14},{18,... | collective-permute-start | bytes 221192 | tf_op jit(solution)/shard_map/ppermute | solution.py:70
  112.4 3.7 %collective-permute-done.1 = bf16[288,128]{1,0:T(8,128)(2,1)S(1)} collective-permute-done((bf16[288,128]{1,0:T(8,128)(2,1)S(1)}, bf16[288,128]{1,0:T(8,128)(2,1)S(1)}, u32[]{:S(2)}, u32[]{:S(2)}) %collective-permute-start.1) | collective-permute-done | bytes 73760 | tf_op jit(solution)/shard_map/ppermute | solution.py:68
  116.1 4.4 %collective-permute-start.9 = (bf16[288,128]{1,0:T(8,128)(2,1)S(1)}, bf16[288,128]{1,0:T(8,128)(2,1)S(1)}, u32[]{:S(2)}, u32[]{:S(2)}) collective-permute-start(bf16[288,128]{1,0:T(8,128)(2,1)S(1)} %collective-permute-done.8), channel_id=1, source_target_pairs={{0,30},{2,0},{4,2},{6,4},{8,6},{10,8},{12,10},{14,12},{16,14},{18,... | collective-permute-start | bytes 221192 | tf_op jit(solution)/shard_map/ppermute | solution.py:70
  120.6 3.7 %collective-permute-done.2 = bf16[288,128]{1,0:T(8,128)(2,1)S(1)} collective-permute-done((bf16[288,128]{1,0:T(8,128)(2,1)S(1)}, bf16[288,128]{1,0:T(8,128)(2,1)S(1)}, u32[]{:S(2)}, u32[]{:S(2)}) %collective-permute-start.2) | collective-permute-done | bytes 73760 | tf_op jit(solution)/shard_map/ppermute | solution.py:68
  124.3 4.4 %collective-permute-start.10 = (bf16[288,128]{1,0:T(8,128)(2,1)S(1)}, bf16[288,128]{1,0:T(8,128)(2,1)S(1)}, u32[]{:S(2)}, u32[]{:S(2)}) collective-permute-start(bf16[288,128]{1,0:T(8,128)(2,1)S(1)} %collective-permute-done.9), channel_id=1, source_target_pairs={{0,30},{2,0},{4,2},{6,4},{8,6},{10,8},{12,10},{14,12},{16,14},{18,... | collective-permute-start | bytes 221192 | tf_op jit(solution)/shard_map/ppermute | solution.py:70
  128.7 2.0 collective-permute-done.3
  130.8 4.5 %collective-permute-start.11 = (bf16[288,128]{1,0:T(8,128)(2,1)S(1)}, bf16[288,128]{1,0:T(8,128)(2,1)S(1)}, u32[]{:S(2)}, u32[]{:S(2)}) collective-permute-start(bf16[288,128]{1,0:T(8,128)(2,1)S(1)} %collective-permute-done.10), channel_id=1, source_target_pairs={{0,30},{2,0},{4,2},{6,4},{8,6},{10,8},{12,10},{14,12},{16,14},{18,... | collective-permute-start | bytes 221192 | tf_op jit(solution)/shard_map/ppermute | solution.py:70
  135.3 2.1 collective-permute-done.4
  137.4 1.5 collective-permute-done.11
  138.9 4.6 %collective-permute-start.12 = (bf16[288,128]{1,0:T(8,128)(2,1)S(1)}, bf16[288,128]{1,0:T(8,128)(2,1)S(1)}, u32[]{:S(2)}, u32[]{:S(2)}) collective-permute-start(bf16[288,128]{1,0:T(8,128)(2,1)S(1)} %collective-permute-done.11), channel_id=1, source_target_pairs={{0,30},{2,0},{4,2},{6,4},{8,6},{10,8},{12,10},{14,12},{16,14},{18,... | collective-permute-start | bytes 221192 | tf_op jit(solution)/shard_map/ppermute | solution.py:70
  143.6 2.0 collective-permute-done.5
  145.6 1.6 collective-permute-done.12
  147.1 4.6 %collective-permute-start.13 = (bf16[288,128]{1,0:T(8,128)(2,1)S(1)}, bf16[288,128]{1,0:T(8,128)(2,1)S(1)}, u32[]{:S(2)}, u32[]{:S(2)}) collective-permute-start(bf16[288,128]{1,0:T(8,128)(2,1)S(1)} %collective-permute-done.12), channel_id=1, source_target_pairs={{0,30},{2,0},{4,2},{6,4},{8,6},{10,8},{12,10},{14,12},{16,14},{18,... | collective-permute-start | bytes 221192 | tf_op jit(solution)/shard_map/ppermute | solution.py:70
  151.7 2.0 collective-permute-done.6
  154.4 0.7 collective-permute-done.13
  155.1 4.6 %collective-permute-start.14 = (bf16[288,128]{1,0:T(8,128)(2,1)S(1)}, bf16[288,128]{1,0:T(8,128)(2,1)S(1)}, u32[]{:S(2)}, u32[]{:S(2)}) collective-permute-start(bf16[288,128]{1,0:T(8,128)(2,1)S(1)} %collective-permute-done.13), channel_id=1, source_target_pairs={{0,30},{2,0},{4,2},{6,4},{8,6},{10,8},{12,10},{14,12},{16,14},{18,... | collective-permute-start | bytes 221192 | tf_op jit(solution)/shard_map/ppermute | solution.py:70
  159.7 1.2 collective-permute-done.7
  161.0 0.6 constant_dynamic-update-slice_fusion.31
  163.5 0.6 constant_dynamic-update-slice_fusion.27
  165.4 0.6 constant_dynamic-update-slice_fusion.24
  166.1 0.6 constant_dynamic-update-slice_fusion.23
  168.0 0.6 constant_dynamic-update-slice_fusion.20
  168.6 0.6 constant_dynamic-update-slice_fusion.19
  170.5 0.6 constant_dynamic-update-slice_fusion.16
  171.8 0.6 constant_dynamic-update-slice_fusion.14
  172.5 0.6 constant_dynamic-update-slice_fusion.13
  181.4 7.0 %convolution_add_fusion = f32[288,512]{1,0:T(8,128)S(1)} fusion(bf16[8192,512]{1,0:T(8,128)(2,1)} %all-gather.8.cloned.1.call-done, f32[512]{0:T(512)S(1)} %convert_element_type.56, bf16[288,8192]{1,0:T(8,128)(2,1)} %param.11, f32[8192]{0:T(1024)S(1)} %convert_element_type.51, f32[288]{0:T(512)S(1)} %add_rsqrt_fusion), kind=kOutput, calls=%fused_computation.23 | convolution fusion | flops 2425503744 | bytes 13732992 | tf_op jit(solution)/shard_map/dot_general | solution.py:33
  189.4 28.0 %all-gather.12.cloned.1.call-done = bf16[4608,128]{1,0:T(8,128)(2,1)} async-done(((bf16[288,128]{1,0:T(8,128)(2,1)}), bf16[4608,128]{1,0:T(8,128)(2,1)}) %all-gather.12.cloned.1.call-update) | async-done | bytes 1179664 | tf_op jit(solution)/shard_map/all_gather | solution.py:73
  217.4 19.7 %conditional.1 = (f32[4,288]{1,0:T(4,128)S(1)}, f32[4,288,128]{2,1,0:T(8,128)S(1)}) conditional(s32[]{:T(128)} %convert_element_type.49, () %tuple.23, (s32[]{:T(128)}, s32[288]{0:T(512)S(1)}, s32[]{:T(128)}, bf16[9216,128]{1,0:T(8,128)(2,1)}, bf16[4,288,128]{2,1,0:T(8,128)(2,1)S(1)}, /*index=5*/bf16[4608,128]{1,0:T(8,128)(2,1)}) %tuple.24), branch_computations={%region_1.2_spmd, %region_2.5_spmd} | conditional | flops 2777627648 | bytes 72284696 | solution.py:98
  217.4 0.8 iota_compare_fusion
  218.1 5.7 %fusion.2 = (f32[4,288]{1,0:T(4,128)S(1)}, f32[4608,4,288]{0,2,1:T(8,128)S(1)}) fusion(pred[288,4608]{1,0:T(8,128)(4,1)S(1)} %iota_compare_fusion, bf16[4,288,128]{2,1,0:T(8,128)(2,1)S(1)} %get-tuple-element.115, bf16[9216,128]{1,0:T(8,128)(2,1)} %get-tuple-element.113, s32[]{:T(128)S(6)} %select_n.25), kind=kOutput, calls=%fused_computation.4 | convolution fusion | flops 1374878592 | bytes 24039940 | tf_op jit(solution)/shard_map/cond/branch_1_fun/hqd,kd->hqk/dot_general | solution.py:78
  223.9 6.6 %fusion.3 = f32[4,288,128]{2,1,0:T(8,128)S(1)} fusion(f32[4608,4,288]{0,2,1:T(8,128)S(1)} %get-tuple-element.122, f32[4,288]{1,0:T(4,128)S(1)} %broadcast_maximum_fusion, pred[288,4608]{1,0:T(8,128)(4,1)S(1)} %iota_compare_fusion, bf16[4608,128]{1,0:T(8,128)(2,1)} %get-tuple-element.116), kind=kOutput, calls=%fused_computation.5 | convolution fusion | flops 1380188160 | bytes 24334848 | tf_op jit(solution)/shard_map/cond/branch_1_fun/hqk,kd->hqd/dot_general | solution.py:87
  230.5 6.6 %fusion.1 = f32[4,288]{1,0:T(4,128)S(1)} fusion(f32[4608,4,288]{0,2,1:T(8,128)S(1)} %get-tuple-element.122, f32[4,288]{1,0:T(4,128)S(1)} %broadcast_maximum_fusion, pred[288,4608]{1,0:T(8,128)(4,1)S(1)} %iota_compare_fusion), kind=kLoop, calls=%fused_computation.3 | loop fusion | flops 21232512 | bytes 22569984 | tf_op jit(solution)/shard_map/cond/branch_1_fun/reduce_sum | solution.py:86
  237.1 58.9 %all-gather.14.cloned.1.call-done = bf16[512,8192]{1,0:T(8,128)(2,1)} async-done(((bf16[512,512]{1,0:T(8,128)(2,1)}), bf16[512,8192]{1,0:T(8,128)(2,1)}) %all-gather.14.cloned.1.call-update) | async-done | bytes 8388624 | tf_op jit(solution)/shard_map/all_gather | solution.py:103
  296.0 7.8 %convolution_convert_fusion = bf16[288,8192]{1,0:T(8,128)(2,1)} fusion(bf16[512,8192]{1,0:T(8,128)(2,1)} %all-gather.14.cloned.1.call-done, f32[4,288,128]{2,1,0:T(8,128)S(1)} %get-tuple-element.119, f32[4,288]{1,0:T(4,128)S(1)} %get-tuple-element.120), kind=kOutput, calls=%fused_computation.19 | convolution fusion | flops 2418573312 | bytes 13701632 | tf_op jit(solution)/shard_map/dot_general | solution.py:101
  303.8 58.4 %reduce-scatter.2.cloned.1.call-done = bf16[144,8192]{1,0:T(8,128)(2,1)} async-done(((bf16[288,8192]{1,0:T(8,128)(2,1)}), bf16[144,8192]{1,0:T(8,128)(2,1)}) %reduce-scatter.2.cloned.1.call-update) | async-done | bytes 2359312 | tf_op jit(solution)/shard_map/reduce_scatter | solution.py:106
  (63 shorter events, 17.4 us)
Async XLA Ops:
  6.5 47.2 %all-gather.10.cloned.1.call-start = ((), (), s32[]{:S(2)}) async-start(), calls=%async_computation.3 | async-start | bytes 2228224 | tf_op jit(solution)/shard_map/all_gather | solution.py:43
  7.3 88.8 %all-gather.6.cloned.1.call-start = ((), (), s32[]{:S(2)}) async-start(), calls=%async_computation.1 | async-start | bytes 2228224 | tf_op jit(solution)/shard_map/all_gather | solution.py:39
  8.0 173.4 %all-gather.8.cloned.1.call-start = ((), (), s32[]{:S(2)}) async-start(), calls=%async_computation.2 | async-start | bytes 8912896 | tf_op jit(solution)/shard_map/all_gather | solution.py:35
  8.7 208.6 %all-gather.12.cloned.1.call-start = ((), (), s32[]{:S(2)}) async-start(), calls=%async_computation.4 | async-start | bytes 1253376 | tf_op jit(solution)/shard_map/all_gather | solution.py:73
  13.5 46.0 %copy-start.1 = (bf16[128]{0:T(256)(128)(2,1)S(1)}, bf16[128]{0:T(256)(128)(2,1)}, u32[]{:S(2)}) copy-start(bf16[128]{0:T(256)(128)(2,1)} %param.17) | copy-start | bytes 772
  58.9 237.1 %all-gather.14.cloned.1.call-start = ((), (), s32[]{:S(2)}) async-start(), calls=%async_computation.5 | async-start | bytes 8912896 | tf_op jit(solution)/shard_map/all_gather | solution.py:103
  59.5 302.8 %reduce-scatter.2.cloned.1.call-start = ((), (), s32[]{:S(2)}) async-start(), calls=%async_computation.6 | async-start | bytes 7077888 | tf_op jit(solution)/shard_map/reduce_scatter | solution.py:106
  59.6 94.8 %copy-start = (bf16[512]{0:T(512)(128)(2,1)S(1)}, bf16[512]{0:T(512)(128)(2,1)}, u32[]{:S(2)}) copy-start(bf16[512]{0:T(512)(128)(2,1)} %param.16) | copy-start | bytes 3076
  101.4 6.5 %collective-permute-start = (bf16[288,128]{1,0:T(8,128)(2,1)S(1)}, bf16[288,128]{1,0:T(8,128)(2,1)S(1)}, u32[]{:S(2)}, u32[]{:S(2)}) collective-permute-start(bf16[288,128]{1,0:T(8,128)(2,1)S(1)} %maximum_bitcast_fusion.1), channel_id=1, source_target_pairs={{0,2},{2,4},{4,6},{6,8},{8,10},{10,12},{12,14},{14,16},{16,18},{18... | collective-permute-start | bytes 221192 | tf_op jit(solution)/shard_map/ppermute | solution.py:68
  107.9 8.2 %collective-permute-start.1 = (bf16[288,128]{1,0:T(8,128)(2,1)S(1)}, bf16[288,128]{1,0:T(8,128)(2,1)S(1)}, u32[]{:S(2)}, u32[]{:S(2)}) collective-permute-start(bf16[288,128]{1,0:T(8,128)(2,1)S(1)} %collective-permute-done), channel_id=1, source_target_pairs={{0,2},{2,4},{4,6},{6,8},{8,10},{10,12},{12,14},{14,16},{16,18},{18... | collective-permute-start | bytes 221192 | tf_op jit(solution)/shard_map/ppermute | solution.py:68
  107.9 8.2 %collective-permute-start.8 = (bf16[288,128]{1,0:T(8,128)(2,1)S(1)}, bf16[288,128]{1,0:T(8,128)(2,1)S(1)}, u32[]{:S(2)}, u32[]{:S(2)}) collective-permute-start(bf16[288,128]{1,0:T(8,128)(2,1)S(1)} %maximum_bitcast_fusion.1), channel_id=1, source_target_pairs={{0,30},{2,0},{4,2},{6,4},{8,6},{10,8},{12,10},{14,12},{16,14},{18,... | collective-permute-start | bytes 221192 | tf_op jit(solution)/shard_map/ppermute | solution.py:70
  116.1 8.2 %collective-permute-start.2 = (bf16[288,128]{1,0:T(8,128)(2,1)S(1)}, bf16[288,128]{1,0:T(8,128)(2,1)S(1)}, u32[]{:S(2)}, u32[]{:S(2)}) collective-permute-start(bf16[288,128]{1,0:T(8,128)(2,1)S(1)} %collective-permute-done.1), channel_id=1, source_target_pairs={{0,2},{2,4},{4,6},{6,8},{8,10},{10,12},{12,14},{14,16},{16,18},{18... | collective-permute-start | bytes 221192 | tf_op jit(solution)/shard_map/ppermute | solution.py:68
  116.1 8.2 %collective-permute-start.9 = (bf16[288,128]{1,0:T(8,128)(2,1)S(1)}, bf16[288,128]{1,0:T(8,128)(2,1)S(1)}, u32[]{:S(2)}, u32[]{:S(2)}) collective-permute-start(bf16[288,128]{1,0:T(8,128)(2,1)S(1)} %collective-permute-done.8), channel_id=1, source_target_pairs={{0,30},{2,0},{4,2},{6,4},{8,6},{10,8},{12,10},{14,12},{16,14},{18,... | collective-permute-start | bytes 221192 | tf_op jit(solution)/shard_map/ppermute | solution.py:70
  124.3 6.5 %collective-permute-start.3 = (bf16[288,128]{1,0:T(8,128)(2,1)S(1)}, bf16[288,128]{1,0:T(8,128)(2,1)S(1)}, u32[]{:S(2)}, u32[]{:S(2)}) collective-permute-start(bf16[288,128]{1,0:T(8,128)(2,1)S(1)} %collective-permute-done.2), channel_id=1, source_target_pairs={{0,2},{2,4},{4,6},{6,8},{8,10},{10,12},{12,14},{14,16},{16,18},{18... | collective-permute-start | bytes 221192 | tf_op jit(solution)/shard_map/ppermute | solution.py:68
  124.3 6.5 %collective-permute-start.10 = (bf16[288,128]{1,0:T(8,128)(2,1)S(1)}, bf16[288,128]{1,0:T(8,128)(2,1)S(1)}, u32[]{:S(2)}, u32[]{:S(2)}) collective-permute-start(bf16[288,128]{1,0:T(8,128)(2,1)S(1)} %collective-permute-done.9), channel_id=1, source_target_pairs={{0,30},{2,0},{4,2},{6,4},{8,6},{10,8},{12,10},{14,12},{16,14},{18,... | collective-permute-start | bytes 221192 | tf_op jit(solution)/shard_map/ppermute | solution.py:70
  130.8 6.6 %collective-permute-start.4 = (bf16[288,128]{1,0:T(8,128)(2,1)S(1)}, bf16[288,128]{1,0:T(8,128)(2,1)S(1)}, u32[]{:S(2)}, u32[]{:S(2)}) collective-permute-start(bf16[288,128]{1,0:T(8,128)(2,1)S(1)} %collective-permute-done.3), channel_id=1, source_target_pairs={{0,2},{2,4},{4,6},{6,8},{8,10},{10,12},{12,14},{14,16},{16,18},{18... | collective-permute-start | bytes 221192 | tf_op jit(solution)/shard_map/ppermute | solution.py:68
  130.8 8.2 %collective-permute-start.11 = (bf16[288,128]{1,0:T(8,128)(2,1)S(1)}, bf16[288,128]{1,0:T(8,128)(2,1)S(1)}, u32[]{:S(2)}, u32[]{:S(2)}) collective-permute-start(bf16[288,128]{1,0:T(8,128)(2,1)S(1)} %collective-permute-done.10), channel_id=1, source_target_pairs={{0,30},{2,0},{4,2},{6,4},{8,6},{10,8},{12,10},{14,12},{16,14},{18,... | collective-permute-start | bytes 221192 | tf_op jit(solution)/shard_map/ppermute | solution.py:70
  137.4 8.2 %collective-permute-start.5 = (bf16[288,128]{1,0:T(8,128)(2,1)S(1)}, bf16[288,128]{1,0:T(8,128)(2,1)S(1)}, u32[]{:S(2)}, u32[]{:S(2)}) collective-permute-start(bf16[288,128]{1,0:T(8,128)(2,1)S(1)} %collective-permute-done.4), channel_id=1, source_target_pairs={{0,2},{2,4},{4,6},{6,8},{8,10},{10,12},{12,14},{14,16},{16,18},{18... | collective-permute-start | bytes 221192 | tf_op jit(solution)/shard_map/ppermute | solution.py:68
  138.9 8.2 %collective-permute-start.12 = (bf16[288,128]{1,0:T(8,128)(2,1)S(1)}, bf16[288,128]{1,0:T(8,128)(2,1)S(1)}, u32[]{:S(2)}, u32[]{:S(2)}) collective-permute-start(bf16[288,128]{1,0:T(8,128)(2,1)S(1)} %collective-permute-done.11), channel_id=1, source_target_pairs={{0,30},{2,0},{4,2},{6,4},{8,6},{10,8},{12,10},{14,12},{16,14},{18,... | collective-permute-start | bytes 221192 | tf_op jit(solution)/shard_map/ppermute | solution.py:70
  145.6 8.2 %collective-permute-start.6 = (bf16[288,128]{1,0:T(8,128)(2,1)S(1)}, bf16[288,128]{1,0:T(8,128)(2,1)S(1)}, u32[]{:S(2)}, u32[]{:S(2)}) collective-permute-start(bf16[288,128]{1,0:T(8,128)(2,1)S(1)} %collective-permute-done.5), channel_id=1, source_target_pairs={{0,2},{2,4},{4,6},{6,8},{8,10},{10,12},{12,14},{14,16},{16,18},{18... | collective-permute-start | bytes 221192 | tf_op jit(solution)/shard_map/ppermute | solution.py:68
  147.1 7.9 %collective-permute-start.13 = (bf16[288,128]{1,0:T(8,128)(2,1)S(1)}, bf16[288,128]{1,0:T(8,128)(2,1)S(1)}, u32[]{:S(2)}, u32[]{:S(2)}) collective-permute-start(bf16[288,128]{1,0:T(8,128)(2,1)S(1)} %collective-permute-done.12), channel_id=1, source_target_pairs={{0,30},{2,0},{4,2},{6,4},{8,6},{10,8},{12,10},{14,12},{16,14},{18,... | collective-permute-start | bytes 221192 | tf_op jit(solution)/shard_map/ppermute | solution.py:70
  153.8 7.2 %collective-permute-start.7 = (bf16[288,128]{1,0:T(8,128)(2,1)S(1)}, bf16[288,128]{1,0:T(8,128)(2,1)S(1)}, u32[]{:S(2)}, u32[]{:S(2)}) collective-permute-start(bf16[288,128]{1,0:T(8,128)(2,1)S(1)} %collective-permute-done.6), channel_id=1, source_target_pairs={{0,2},{2,4},{4,6},{6,8},{8,10},{10,12},{12,14},{14,16},{16,18},{18... | collective-permute-start | bytes 221192 | tf_op jit(solution)/shard_map/ppermute | solution.py:68
  155.1 15.5 %collective-permute-start.14 = (bf16[288,128]{1,0:T(8,128)(2,1)S(1)}, bf16[288,128]{1,0:T(8,128)(2,1)S(1)}, u32[]{:S(2)}, u32[]{:S(2)}) collective-permute-start(bf16[288,128]{1,0:T(8,128)(2,1)S(1)} %collective-permute-done.13), channel_id=1, source_target_pairs={{0,30},{2,0},{4,2},{6,4},{8,6},{10,8},{12,10},{14,12},{16,14},{18,... | collective-permute-start | bytes 221192 | tf_op jit(solution)/shard_map/ppermute | solution.py:70
Sparse Core Ops, SparseCore 0:
  9.5 44.1 all-gather.9
  55.9 40.1 all-gather.5
  98.2 79.0 all-gather.7
  179.4 37.9 all-gather.11
  219.4 76.5 all-gather.13
  304.0 58.2 reduce-scatter.1
